TPU v7x, 256 devices: a whole 4x4x8 slice. The times are simulated.
256 devices in a mesh: ka: 32 (over z_hi, x, y), ga: 8 (over z_lo, core).
Axes of the slice: x: 4, y: 4, z: 8 (z_hi: 2, z_lo: 4; z = z_hi * 4 + z_lo), core: 2. Of those that a mesh axis runs over, the one named last changes fastest.
Arguments:
- psi: bfloat16 [32, 2, 128, 2048], P('ka', None, None, 'ga'), may hold values from -0.62890625 to 0.62890625
- dvscf: bfloat16 [96, 2, 2048], P(None, None, 'ga'), may hold values from -6 to 6
- kq_map: int32 [32], P('ka'), may hold values from 0 to 31, each once
Outputs:
- coupling: float32 [96, 32, 2, 128, 128], P('ga', 'ka')
Inputs may be any that keep to these rules, and one draw needn't show every extreme that they name: kq_map is a permutation of the k-points 0 to 31.
All inputs are finite; a program needn't handle non-finite values.
Results may differ from a plain program's by a relative error of at most 0.0029.
Values may be sent and summed in bfloat16 or wider, within the bound.
No kernel may reach another device: no remote copies, remote signals or barrier semaphores. Data moves between devices by JAX's collectives and lax.ppermute only.
A program may use at most 128 MiB of HBM per device.

v0:
```python
import jax
import jax.numpy as jnp
from jax import lax
from jax.sharding import Mesh
from jax.sharding import PartitionSpec as P

KA = ("ka_0", "ka_1", "ka_2")


def joined_along(blocks, dim):
    dims = list(blocks.shape[1:])
    dims[dim] *= blocks.shape[0]
    return jnp.moveaxis(blocks, 0, dim).reshape(dims)


def gather_in_order(value, axes, sequence):
    blocks = value[None]
    for k in sequence:
        blocks = lax.all_gather(blocks, axes[k], axis=0, tiled=True)
    current = [lax.axis_size(axes[k]) for k in reversed(sequence)]
    blocks = blocks.reshape(*current, *value.shape)
    turned = sorted(range(len(sequence)), key=lambda place: sequence[len(sequence) - 1 - place])
    return blocks.transpose(*turned, *range(len(sequence), blocks.ndim)).reshape(-1, *value.shape)


def gathered_by_axis(value, axes, sequence, dim):
    return joined_along(gather_in_order(value, axes, sequence), dim)


def in_one_piece(arrays, axis, dim, along):
    ends, at = ([], 0)
    for a in arrays[:-1]:
        at += a.shape[along]
        ends.append(at)
    both = jnp.concatenate(arrays, axis=along)
    return tuple(jnp.split(lax.all_gather(both, axis, axis=dim, tiled=True), ends, axis=along))


def block_modes(left, wave_real, wave_imag, potential):
    dv_real = potential[:, 0].astype(jnp.float32)[:, None, None, :]
    dv_imag = potential[:, 1].astype(jnp.float32)[:, None, None, :]
    prod_real = (dv_real * wave_real[None] - dv_imag * wave_imag[None]).astype(jnp.bfloat16)
    prod_imag = (dv_real * wave_imag[None] + dv_imag * wave_real[None]).astype(jnp.bfloat16)
    right = jnp.stack(
        [
            jnp.concatenate([prod_real, prod_imag], axis=-1),
            jnp.concatenate([prod_imag, -prod_real], axis=-1),
        ],
        axis=2,
    )
    return jnp.einsum("kmr,ukcnr->ukcmn", left, right, preferred_element_type=jnp.float32)


def mode_block(left, wave, dv_block):
    wave_real = wave[:, 0].astype(jnp.float32)
    wave_imag = wave[:, 1].astype(jnp.float32)
    return block_modes(left, wave_real, wave_imag, dv_block)


def stack_left(other):
    return jnp.concatenate([other[:, 0], other[:, 1]], axis=-1)


def body(psi, dvscf, kq_map):
    piece = gathered_by_axis(psi, KA, (0, 1, 2), 0)
    within = (kq_map >= 0) & (kq_map < piece.shape[0])
    clipped = jnp.clip(kq_map, 0, piece.shape[0] - 1)
    taken = jnp.take(piece, clipped, axis=0)
    phi = jnp.where(within[:, None, None, None], taken, jnp.zeros_like(psi))
    dv_modes = lax.all_to_all(dvscf, "ga", split_axis=0, concat_axis=2, tiled=True)
    wave_piece, other_piece = in_one_piece((psi, phi), "ga", 3, 0)
    return mode_block(stack_left(other_piece), wave_piece, dv_modes)


def solution(mesh):
    finer = Mesh(mesh.devices.reshape(2, 4, 4, mesh.shape["ga"]), ("ka_0", "ka_1", "ka_2", "ga"))
    in_specs = (P(KA, None, None, "ga"), P(None, None, "ga"), P(KA))
    out_specs = P("ga", KA, None, None, None)
    return jax.shard_map(body, mesh=finer, in_specs=in_specs, out_specs=out_specs, check_vma=False)
```

profile of v0, /device:TPU:1, one launch (start us, length us, event | category | flops | bytes accessed | tf_op | source)
XLA Modules:
  0.0 180.3 jit_solution(7627843267096762044)
XLA Ops:
  6.5 0.0 all-gather.9.cloned.1.call-start
  6.5 13.4 %all-gather = bf16[2,2,128,256]{3,2,1,0:T(8,128)(2,1)} all-gather(bf16[1,2,128,256]{3,2,1,0:T(8,128)(2,1)} %param.3), channel_id=2, replica_groups=mesh['ka_0'=2,'ka_1'=4,'ka_2'=4,'ga'=8] {'ka_0'}, dimensions={0}, use_global_device_ids=true | all-gather | bytes 393216 | tf_op jit(solution)/shard_map/all_gather | solution.py:19
  19.9 0.0 all-gather.9.cloned.1.call-update
  19.9 0.0 all-gather.11.cloned.1.call-start
  20.0 27.5 %all-gather.9.cloned.1.call-done = bf16[8,2,128,256]{3,2,1,0:T(8,128)(2,1)} async-done(((bf16[2,2,128,256]{3,2,1,0:T(8,128)(2,1)}), bf16[8,2,128,256]{3,2,1,0:T(8,128)(2,1)}) %all-gather.9.cloned.1.call-update) | async-done | bytes 1048592 | tf_op jit(solution)/shard_map/all_gather | solution.py:19
  47.5 0.0 all-gather.11.cloned.1.call-update
  47.6 0.0 all-gather.7.cloned.1.call-start
  48.3 54.2 %all-gather.11.cloned.1.call-done = bf16[32,2,128,256]{3,2,1,0:T(8,128)(2,1)} async-done(((bf16[8,2,128,256]{3,2,1,0:T(8,128)(2,1)}), bf16[32,2,128,256]{3,2,1,0:T(8,128)(2,1)}) %all-gather.11.cloned.1.call-update) | async-done | bytes 4194320 | tf_op jit(solution)/shard_map/all_gather | solution.py:19
  102.5 2.5 %copy.13 = bf16[4,4,2,1,2,128,256]{6,5,4,0,1,2,3:T(8,128)(2,1)S(1)} copy(bf16[4,4,2,1,2,128,256]{6,5,4,2,1,0,3:T(8,128)(2,1)} %bitcast.54) | data formatting | bytes 8388608 | tf_op jit(solution)/shard_map/reshape | solution.py:21
  104.9 1.6 pad_maximum_fusion
  106.6 0.0 all-gather.7.cloned.1.call-update
  106.6 11.0 %all_to_all.18 = bf16[96,2,256]{2,1,0:T(2,128)(2,1)S(1)} all-to-all(bf16[96,2,256]{2,1,0:T(2,128)(2,1)} %param.4), channel_id=1, replica_groups=mesh['ka_0'=2,'ka_1'=4,'ka_2'=4,'ga'=8] {'ga'}, dimensions={0} | all-to-all | bytes 196608 | tf_op jit(solution)/shard_map/all_to_all | solution.py:70
  117.7 0.1 slice_convert_fusion.1
  117.8 0.1 copy_bitcast_fusion
  117.9 28.4 %all-gather.7.cloned.1.call-done = bf16[2,2,128,2048]{3,2,1,0:T(8,128)(2,1)} async-done(((bf16[2,2,128,256]{3,2,1,0:T(8,128)(2,1)}), bf16[2,2,128,2048]{3,2,1,0:T(8,128)(2,1)}) %all-gather.7.cloned.1.call-update) | async-done | bytes 2097168 | tf_op jit(solution)/shard_map/all_gather | solution.py:36
  146.3 2.8 %slice_bitcast_fusion.1 = (bf16[1,128,2048]{2,1,0:T(8,128)(2,1)}, bf16[1,128,2048]{2,1,0:T(8,128)(2,1)}, f32[128,2048]{1,0:T(8,128)S(1)}, f32[128,2048]{1,0:T(8,128)S(1)}) fusion(bf16[2,2,128,2048]{3,2,1,0:T(8,128)(2,1)} %all-gather.7.cloned.1.call-done), kind=kLoop, calls=%fused_computation.13 | loop fusion | flops 524288 | bytes 5242880 | tf_op jit(solution)/shard_map/squeeze | solution.py:61
  149.1 1.9 %fusion.10 = bf16[12,1,128,2048]{3,2,0,1:T(8,128)(2,1)S(1)} fusion(f32[128,2048]{1,0:T(8,128)S(1)} %get-tuple-element.22, f32[12,2048]{1,0:T(8,128)S(1)} %get-tuple-element.26, f32[128,2048]{1,0:T(8,128)S(1)} %get-tuple-element.23, f32[12,2048]{1,0:T(8,128)S(1)} %get-tuple-element.27), kind=kLoop, calls=%fused_computation.27 | loop fusion | flops 15728640 | bytes 8585216 | tf_op jit(solution)/shard_map/neg | solution.py:47
  151.0 3.4 %subtract_convert_fusion = (bf16[12,1,128,2048]{3,2,0,1:T(8,128)(2,1)S(1)}, bf16[12,1,128,2048]{3,2,0,1:T(8,128)(2,1)S(1)}) fusion(f32[128,2048]{1,0:T(8,128)S(1)} %get-tuple-element.22, f32[12,2048]{1,0:T(8,128)S(1)} %get-tuple-element.26, f32[128,2048]{1,0:T(8,128)S(1)} %get-tuple-element.23, f32[12,2048]{1,0:T(8,128)S(1)} %get-tuple-element.27), kind=kLoop, calls=%fused_computation.7 | loop fusion | flops 25165824 | bytes 14876672 | tf_op jit(solution)/shard_map/convert_element_type | solution.py:42
  154.4 5.5 %maximum_bitcast_fusion.2 = (bf16[12,1,1,128,4096]{4,3,2,0,1:T(8,128)(2,1)S(1)}, bf16[12,1,1,128,4096]{4,3,2,0,1:T(8,128)(2,1)}) fusion(bf16[12,1,128,2048]{3,2,0,1:T(8,128)(2,1)S(1)} %get-tuple-element.19, bf16[12,1,128,2048]{3,2,0,1:T(8,128)(2,1)S(1)} %get-tuple-element.18, bf16[12,1,128,2048]{3,2,0,1:T(8,128)(2,1)S(1)} %fusion.10), kind=kLoop, calls=%fused_computation.4 | loop fusion | flops 50331648 | bytes 44040192 | tf_op jit(solution)/shard_map/stack | solution.py:44
  159.9 10.8 %fusion.3 = f32[12,1,2,128,128]{3,4,2,0,1:T(8,128)} fusion(bf16[12,1,1,128,4096]{4,3,2,0,1:T(8,128)(2,1)} %get-tuple-element.17, bf16[12,1,1,128,4096]{4,3,2,0,1:T(8,128)(2,1)S(1)} %get-tuple-element.16, bf16[1,128,2048]{2,1,0:T(8,128)(2,1)} %get-tuple-element.21, bf16[1,128,2048]{2,1,0:T(8,128)(2,1)} %get-tuple-element.20), kind=kOutput, calls=%fused_computation.8 | convolution fusion | flops 3235905536 | bytes 27787264 | tf_op jit(solution)/shard_map/kmr,ukcnr->ukcmn/dot_general | solution.py:51
  170.7 3.0 %copy.15 = f32[12,1,2,128,128]{4,3,2,1,0:T(8,128)} copy(f32[12,1,2,128,128]{3,4,2,0,1:T(8,128)} %fusion.3) | data formatting | bytes 3145728 | tf_op jit(solution)/shard_map/kmr,ukcnr->ukcmn/transpose | solution.py:51
  (3 shorter events, 0.1 us)
Async XLA Ops:
  6.5 41.0 %all-gather.9.cloned.1.call-start = ((), (), s32[]{:S(2)}) async-start(), calls=%async_computation.2 | async-start | bytes 1310720 | tf_op jit(solution)/shard_map/all_gather | solution.py:19
  19.9 82.5 %all-gather.11.cloned.1.call-start = ((), (), s32[]{:S(2)}) async-start(), calls=%async_computation.3 | async-start | bytes 5242880 | tf_op jit(solution)/shard_map/all_gather | solution.py:19
  47.6 98.7 %all-gather.7.cloned.1.call-start = ((), (), s32[]{:S(2)}) async-start(), calls=%async_computation.1 | async-start | bytes 2359296 | tf_op jit(solution)/shard_map/all_gather | solution.py:36
Sparse Core Ops, SparseCore 0:
  20.1 27.4 all-gather.8
  49.3 53.0 all-gather.10
  106.7 39.5 all-gather.6
where the time goes:
time: 181 us; the launch traced here: 180 us
  waiting for transfers between devices  110 us (61%)
  blocking collectives  24.4 us (13%)
  other arithmetic  15.4 us (9%)
  between operations  13.8 us (8%)
  matrix products  10.8 us (6%)
  local copies, waits for them, and re-layouts  5.59 us (3%)
    all_gather x2, waiting for transfers between devices, gather_in_order(): blocks = lax.all_gather(blocks, axes[k], axis=0, tiled=True)  81.7 us
    all_gather x1, waiting for transfers between devices, in_one_piece(): lax.all_gather(both, axis, axis=dim, tiled=True)  28.4 us
    all_gather x1, blocking collectives, gather_in_order(): blocks = lax.all_gather(blocks, axes[k], axis=0, tiled=True)  13.4 us
    all_to_all x1, blocking collectives, body(): lax.all_to_all(dvscf, 'ga', split_axis=0, concat_axis=2, tiled=True)  11 us
    dot_general x1, matrix products, block_modes(): jnp.einsum('kmr,ukcnr->ukcmn', left, right, preferred_element_type=jnp.fl...  10.8 us
    another operation x1, other arithmetic, block_modes(): jnp.stack([jnp.concatenate([prod_real, prod_imag], axis=-1), jnp.concaten...  5.48 us
  transfers between devices with their start and end apart: 3, of which 3 were waited for; matrix products, arithmetic and copies ran while one was open for 0% of the time, Pallas kernels for 0%

commit v1 on v0

--- a/solution.py
+++ b/solution.py
@@ -16,7 +16,10 @@
 def gather_in_order(value, axes, sequence):
     blocks = value[None]
     for k in sequence:
-        blocks = lax.all_gather(blocks, axes[k], axis=0, tiled=True)
+        n_dev = lax.axis_size(axes[k])
+        pieces = jnp.stack([blocks for _ in range(n_dev)])
+        pieces = lax.all_to_all(pieces, axes[k], split_axis=0, concat_axis=0)
+        blocks = jnp.concatenate(pieces, axis=0)
     current = [lax.axis_size(axes[k]) for k in reversed(sequence)]
     blocks = blocks.reshape(*current, *value.shape)
     turned = sorted(range(len(sequence)), key=lambda place: sequence[len(sequence) - 1 - place])

time: 181 us -> 174 us (0.961)
  waiting for transfers between devices: 110 us -> 67 us
  blocking collectives: 24.4 us -> 52.1 us
  starting transfers between devices: 0.08 us -> 4.88 us
  other arithmetic: 15.4 us -> 17.6 us
    all_gather x2 -> x0, waiting for transfers between devices: 81.7 us -> none  [gather_in_order(): blocks = lax.all_gather(blocks, axes[k], axis=0, tiled=True)]
    all_to_all x0 -> x1, waiting for transfers between devices: none -> 42.9 us  [gather_in_order(): pieces = lax.all_to_all(pieces, axes[k], split_axis=0, concat_axis=0)]
    all_to_all x0 -> x2, blocking collectives: none -> 31.5 us  [gather_in_order(): pieces = lax.all_to_all(pieces, axes[k], split_axis=0, concat_axis=0)]
    all_gather x1 -> x0, blocking collectives: 13.4 us -> none  [gather_in_order(): blocks = lax.all_gather(blocks, axes[k], axis=0, tiled=True)]
    all_to_all x1, blocking collectives: 11 us -> 20.7 us  [body(): lax.all_to_all(dvscf, 'ga', split_axis=0, concat_axis=2, tiled=True)]
    all_to_all x0 -> x1, starting transfers between devices: none -> 4.84 us  [gather_in_order(): pieces = lax.all_to_all(pieces, axes[k], split_axis=0, concat_axis=0)]
    all_gather x1, waiting for transfers between devices: 28.4 us -> 24 us  [in_one_piece(): lax.all_gather(both, axis, axis=dim, tiled=True)]
    another operation x1, other arithmetic: 5.48 us -> 8.68 us  [block_modes(): jnp.stack([jnp.concatenate([prod_real, prod_imag], axis=-1), jnp.concaten...]
  transfers between devices with their start and end apart: 3 -> 2, of which waited for: 3 -> 2; matrix products, arithmetic and copies ran while one was open for 0% -> 0% of each run, Pallas kernels for 0% -> 0%
where the time goes in v1:
time: 174 us
  waiting for transfers between devices  67 us (39%)
  blocking collectives  52.1 us (30%)
  other arithmetic  17.6 us (10%)
  between operations  14.2 us (8%)
  matrix products  11.4 us (7%)
  local copies, waits for them, and re-layouts  6.77 us (4%)
  starting transfers between devices  4.88 us (3%)
    all_to_all x1, waiting for transfers between devices, gather_in_order(): pieces = lax.all_to_all(pieces, axes[k], split_axis=0, concat_axis=0)  42.9 us
    all_to_all x2, blocking collectives, gather_in_order(): pieces = lax.all_to_all(pieces, axes[k], split_axis=0, concat_axis=0)  31.5 us
    all_gather x1, waiting for transfers between devices, in_one_piece(): lax.all_gather(both, axis, axis=dim, tiled=True)  24 us
    all_to_all x1, blocking collectives, body(): lax.all_to_all(dvscf, 'ga', split_axis=0, concat_axis=2, tiled=True)  20.7 us
    dot_general x1, matrix products, block_modes(): jnp.einsum('kmr,ukcnr->ukcmn', left, right, preferred_element_type=jnp.fl...  11.4 us
    another operation x1, other arithmetic, block_modes(): jnp.stack([jnp.concatenate([prod_real, prod_imag], axis=-1), jnp.concaten...  8.68 us
    all_to_all x1, starting transfers between devices, gather_in_order(): pieces = lax.all_to_all(pieces, axes[k], split_axis=0, concat_axis=0)  4.84 us
  transfers between devices with their start and end apart: 2, of which 2 were waited for; matrix products, arithmetic and copies ran while one was open for 0% of the time, Pallas kernels for 0%

profile of v1, /device:TPU:1, one launch (start us, length us, event | category | flops | bytes accessed | tf_op | source)
XLA Modules:
  0.0 174.0 jit_solution(8999547074585566875)
XLA Ops:
  6.5 1.0 pad_maximum_fusion
  7.5 16.8 %all_to_all.33 = bf16[2,1,1,2,128,256]{5,4,3,2,1,0:T(8,128)(2,1)S(1)} all-to-all(bf16[2,1,1,2,128,256]{5,4,3,2,1,0:T(8,128)(2,1)S(1)} %pad_maximum_fusion), channel_id=1, replica_groups=mesh['ka_0'=2,'ka_1'=4,'ka_2'=4,'ga'=8] {'ka_0'}, dimensions={0} | all-to-all | bytes 524288 | tf_op jit(solution)/shard_map/all_to_all | solution.py:21
  24.4 0.1 stack.19
  24.5 0.0 copy-start.1
  24.5 14.7 %all_to_all.34 = bf16[4,2,1,2,128,256]{5,4,3,1,2,0:T(8,128)(2,1)S(1)} all-to-all(bf16[4,2,1,2,128,256]{5,4,3,1,2,0:T(8,128)(2,1)S(1)} %stack.19), channel_id=1, replica_groups=mesh['ka_0'=2,'ka_1'=4,'ka_2'=4,'ga'=8] {'ka_1'}, dimensions={0} | all-to-all | bytes 2097152 | tf_op jit(solution)/shard_map/all_to_all | solution.py:21
  39.1 2.5 %stack.20 = bf16[4,8,1,2,128,256]{5,4,3,1,2,0:T(8,128)(2,1)} broadcast(bf16[8,2,128,256]{3,2,1,0:T(8,128)(2,1)S(1)} %bitcast.57), dimensions={1,3,4,5} | broadcast | bytes 5242880 | tf_op jit(solution)/shard_map/stack | solution.py:20
  41.6 4.8 %all-to-all-start.3 = ((bf16[4,8,1,2,128,256]{5,4,3,1,2,0:T(8,128)(2,1)}), bf16[4,8,1,2,128,256]{5,4,3,1,2,0:T(8,128)(2,1)}, u32[]{:S(2)}, u32[]{:S(2)}) async-start(bf16[4,8,1,2,128,256]{5,4,3,1,2,0:T(8,128)(2,1)} %stack.20), calls=%async_computation.3 | async-start | bytes 8388608 | tf_op jit(solution)/shard_map/all_to_all | solution.py:21
  46.5 0.0 all-gather.2.cloned.1.call-start
  47.2 42.9 %all-to-all-done.3 = bf16[4,8,1,2,128,256]{5,4,3,1,2,0:T(8,128)(2,1)} async-done(((bf16[4,8,1,2,128,256]{5,4,3,1,2,0:T(8,128)(2,1)}), bf16[4,8,1,2,128,256]{5,4,3,1,2,0:T(8,128)(2,1)}, u32[]{:S(2)}, u32[]{:S(2)}) %all-to-all-start.3) | async-done | bytes 4194336 | tf_op jit(solution)/shard_map/all_to_all | solution.py:21
  90.1 2.5 %copy.12 = bf16[2,4,4,1,2,128,256]{6,5,4,2,1,0,3:T(8,128)(2,1)S(1)} copy(bf16[2,4,4,1,2,128,256]{6,5,4,0,1,2,3:T(8,128)(2,1)} %bitcast.8) | data formatting | bytes 8388608 | tf_op jit(solution)/shard_map/transpose | solution.py:26
  92.6 0.0 copy-done
  92.6 0.7 pad_maximum_fusion.1
  93.3 0.0 all-gather.2.cloned.1.call-update
  93.3 0.0 copy-done.1
  93.3 20.7 %all_to_all.35 = bf16[96,2,256]{2,1,0:T(2,128)(2,1)S(1)} all-to-all(bf16[96,2,256]{2,1,0:T(2,128)(2,1)S(1)} %copy-done.1), channel_id=1, replica_groups=mesh['ka_0'=2,'ka_1'=4,'ka_2'=4,'ga'=8] {'ga'}, dimensions={0} | all-to-all | bytes 196608 | tf_op jit(solution)/shard_map/all_to_all | solution.py:73
  114.1 0.1 slice_convert_fusion.1
  114.2 0.1 copy_bitcast_fusion
  114.3 24.0 %all-gather.2.cloned.1.call-done = bf16[2,2,128,2048]{3,2,1,0:T(8,128)(2,1)} async-done(((bf16[2,2,128,256]{3,2,1,0:T(8,128)(2,1)}), bf16[2,2,128,2048]{3,2,1,0:T(8,128)(2,1)}) %all-gather.2.cloned.1.call-update) | async-done | bytes 2097168 | tf_op jit(solution)/shard_map/all_gather | solution.py:39
  138.3 1.8 %slice_bitcast_fusion.1 = (bf16[1,128,2048]{2,1,0:T(8,128)(2,1)S(1)}, bf16[1,128,2048]{2,1,0:T(8,128)(2,1)S(1)}, f32[128,2048]{1,0:T(8,128)S(1)}, f32[128,2048]{1,0:T(8,128)S(1)}) fusion(bf16[2,2,128,2048]{3,2,1,0:T(8,128)(2,1)} %all-gather.2.cloned.1.call-done), kind=kLoop, calls=%fused_computation.13 | loop fusion | flops 524288 | bytes 5242880 | tf_op jit(solution)/shard_map/squeeze | solution.py:64
  140.1 2.0 %fusion.10 = bf16[12,1,128,2048]{3,2,0,1:T(8,128)(2,1)S(1)} fusion(f32[128,2048]{1,0:T(8,128)S(1)} %get-tuple-element.22, f32[12,2048]{1,0:T(8,128)S(1)} %get-tuple-element.26, f32[128,2048]{1,0:T(8,128)S(1)} %get-tuple-element.23, f32[12,2048]{1,0:T(8,128)S(1)} %get-tuple-element.27), kind=kLoop, calls=%fused_computation.28 | loop fusion | flops 15728640 | bytes 8585216 | tf_op jit(solution)/shard_map/neg | solution.py:50
  142.1 3.3 %subtract_convert_fusion = (bf16[12,1,128,2048]{3,2,0,1:T(8,128)(2,1)S(1)}, bf16[12,1,128,2048]{3,2,0,1:T(8,128)(2,1)S(1)}) fusion(f32[128,2048]{1,0:T(8,128)S(1)} %get-tuple-element.22, f32[12,2048]{1,0:T(8,128)S(1)} %get-tuple-element.26, f32[128,2048]{1,0:T(8,128)S(1)} %get-tuple-element.23, f32[12,2048]{1,0:T(8,128)S(1)} %get-tuple-element.27), kind=kLoop, calls=%fused_computation.7 | loop fusion | flops 25165824 | bytes 14876672 | tf_op jit(solution)/shard_map/convert_element_type | solution.py:45
  145.4 8.7 %maximum_bitcast_fusion.2 = (bf16[12,1,1,128,4096]{4,3,2,0,1:T(8,128)(2,1)}, bf16[12,1,1,128,4096]{4,3,2,0,1:T(8,128)(2,1)}) fusion(bf16[12,1,128,2048]{3,2,0,1:T(8,128)(2,1)S(1)} %get-tuple-element.19, bf16[12,1,128,2048]{3,2,0,1:T(8,128)(2,1)S(1)} %get-tuple-element.18, bf16[12,1,128,2048]{3,2,0,1:T(8,128)(2,1)S(1)} %fusion.10), kind=kLoop, calls=%fused_computation.4 | loop fusion | flops 50331648 | bytes 44040192 | tf_op jit(solution)/shard_map/stack | solution.py:47
  154.1 11.4 %fusion.3 = f32[12,1,2,128,128]{3,4,2,0,1:T(8,128)S(1)} fusion(bf16[12,1,1,128,4096]{4,3,2,0,1:T(8,128)(2,1)} %get-tuple-element.17, bf16[12,1,1,128,4096]{4,3,2,0,1:T(8,128)(2,1)} %get-tuple-element.16, bf16[1,128,2048]{2,1,0:T(8,128)(2,1)S(1)} %get-tuple-element.21, bf16[1,128,2048]{2,1,0:T(8,128)(2,1)S(1)} %get-tuple-element.20), kind=kOutput, calls=%fused_computation.8 | convolution fusion | flops 3235905536 | bytes 27787264 | tf_op jit(solution)/shard_map/kmr,ukcnr->ukcmn/dot_general | solution.py:54
  165.5 1.6 copy.14
  (4 shorter events, 0.1 us)
Async XLA Ops:
  24.4 68.2 %copy-start = (bf16[1,2,128,256]{3,2,1,0:T(8,128)(2,1)S(1)}, bf16[1,2,128,256]{3,2,1,0:T(8,128)(2,1)}, u32[]{:S(2)}) copy-start(bf16[1,2,128,256]{3,2,1,0:T(8,128)(2,1)} %param.3) | copy-start | bytes 393220
  24.5 68.9 %copy-start.1 = (bf16[96,2,256]{2,1,0:T(2,128)(2,1)S(1)}, bf16[96,2,256]{2,1,0:T(2,128)(2,1)}, u32[]{:S(2)}) copy-start(bf16[96,2,256]{2,1,0:T(2,128)(2,1)} %param.4) | copy-start | bytes 294916
  41.6 48.5 %all-to-all-start.3 = ((bf16[4,8,1,2,128,256]{5,4,3,1,2,0:T(8,128)(2,1)}), bf16[4,8,1,2,128,256]{5,4,3,1,2,0:T(8,128)(2,1)}, u32[]{:S(2)}, u32[]{:S(2)}) async-start(bf16[4,8,1,2,128,256]{5,4,3,1,2,0:T(8,128)(2,1)} %stack.20), calls=%async_computation.3 | async-start | bytes 8388608 | tf_op jit(solution)/shard_map/all_to_all | solution.py:21
  46.5 91.9 %all-gather.2.cloned.1.call-start = ((), (), s32[]{:S(2)}) async-start(), calls=%async_computation.4 | async-start | bytes 2359296 | tf_op jit(solution)/shard_map/all_gather | solution.py:39
Sparse Core Ops, SparseCore 0:
  93.5 44.8 all-gather.1
